TPU v7x, 32 devices: a whole 2x2x4 slice. The times are simulated.
32 devices in a mesh: rep: 4 (over z), ep: 8 (over y, x, core).
Axes of the slice: x: 2, y: 2, z: 4, core: 2. Of those that a mesh axis runs over, the one named last changes fastest.
Arguments:
- latent_pages: bfloat16 [1536, 36864], P(('rep', 'ep')), may hold values from -4 to 4
- queries: bfloat16 [256, 147456], P(('rep', 'ep')), may hold values from -4 to 4
- residual: bfloat16 [256, 14336], P(('rep', 'ep')), may hold values from -6 to 6
- page_count: int32 [4, 8, 8], P(None, 'ep'), may hold values from 1 to 12, 48 in all within a row
- last_fill: int32 [4, 8, 8], P(None, 'ep'), may hold values from 4 to 64
- page_order: int32 [32, 48], P(('rep', 'ep')), may hold values from 0 to 47, each once within a row
- shed_slots: int32 [4, 8, 2], P(None, 'ep'), may hold values from 0 to 7, as said below
- shed_shift: int32 [8, 2], P('ep'), may hold values from 1 to 3
- expert_ids: int32 [1024, 8], P(('rep', 'ep')), may hold values from 0 to 31, all different within a row; in each aligned block of 32 rows (0 to 31, 32 to 63, ...) at most 16 rows name the same one
- gate_weight: float32 [1024, 8], P(('rep', 'ep')), may hold values from 0.05 to 0.5
- expert_home: int32 [32], replicated, may hold values from 0 to 31, each once
- norm_gain: float32 [3584], replicated, may hold values from 0.1 to 1.9
- value_up: bfloat16 [64, 512, 128], P('ep'), may hold values from -0.59765625 to 0.59765625
- out_weight: bfloat16 [8192, 3584], P('ep'), may hold values from -0.14941406 to 0.14941406
- expert_in: bfloat16 [32, 3584, 1024], P(('rep', 'ep')), may hold values from -0.09375 to 0.09375
- expert_out: bfloat16 [32, 1024, 3584], P(('rep', 'ep')), may hold values from -0.1875 to 0.1875
Outputs:
- attn_proj: bfloat16 [256, 14336], P(('rep', 'ep'))
- layer_out: bfloat16 [256, 14336], P(('rep', 'ep'))
Inputs may be any that keep to these rules, and one draw needn't show every extreme that they name: `shed_slots`: for each device, 2 different slots. `expert_ids`: each row names 8 different experts; in the rows of one device no expert is named by more than 16 rows.
All inputs are finite; a program needn't handle non-finite values.
Results may differ from a plain program's by a relative error of at most 0.015.
Values may be sent and summed in bfloat16 or wider, within the bound.
A program may use at most 192 MiB of HBM per device.

v0:
```python
import functools

import jax
import jax.numpy as jnp
from jax import lax
from jax.experimental import pallas as pl
from jax.experimental.pallas import tpu as pltpu
from jax.sharding import PartitionSpec as P

D = 3584
HEADS = 64
LAT = 512
KVW = 576
VHEAD = 128
TOP = 8
PAGE = 64
SPEC = 4
MAXP = 12
REQ_DEV = 8
PAGES_DEV = 48


SCORE_SCALE = 192.0 ** (-0.5)
NORM_EPS = 0.25
MESH = pl.DeviceIdType.MESH


def shifted(value, axis, steps):
    count = lax.axis_size(axis)
    pairs = [(source, (source + steps) % count) for source in range(count)]
    return lax.ppermute(value, axis, pairs)


def flipped(index, bit):
    width = 1 << bit
    return index + width * (1 - 2 * ((index // width) % 2))


def masked(index, mask):
    for bit in range(mask.bit_length()):
        if mask >> bit & 1:
            index = flipped(index, bit)
    return index


def submasks(bits):
    masks = [0]
    for bit in bits:
        masks = masks + [mask | 1 << bit for mask in masks]
    return masks


def greet(rep_count, bit_count, replica, column):
    barrier = pltpu.get_barrier_semaphore()
    for steps in range(1, rep_count):
        pl.semaphore_signal(barrier, inc=1, device_id=(lax.rem(replica + steps, rep_count), column), device_id_type=MESH)
    for bit in range(bit_count):
        pl.semaphore_signal(barrier, inc=1, device_id=(replica, flipped(column, bit)), device_id_type=MESH)
    pl.semaphore_wait(barrier, rep_count - 1 + bit_count)


def gather_plan(rep_count, bit_count):
    outer = list(range(1, bit_count))
    orders = (outer, outer[::-1])
    names = [("rep", steps) for steps in range(1, rep_count)]
    for half in range(2):
        for stage in range(len(outer)):
            for steps in range(rep_count):
                names += [(half, stage, steps, mask) for mask in submasks(orders[half][:stage])]
        for steps in range(rep_count):
            names += [("core", half, steps, mask) for mask in submasks(outer)]
    return orders, {name: at for at, name in enumerate(names)}


def gather_kernel(rep_count, col_count, in_ref, out_ref, send_sem, recv_sem, local_sem):
    bit_count = col_count.bit_length() - 1
    replica, column = lax.axis_index("rep"), lax.axis_index("ep")
    orders, number = gather_plan(rep_count, bit_count)
    half_rows = in_ref.shape[0] // 2
    greet(rep_count, bit_count, replica, column)

    def block(steps, mask, half):
        rows = slice(None) if half is None else pl.ds(half * half_rows, half_rows)
        origin = lax.rem(replica + rep_count - steps, rep_count)
        return out_ref.at[origin * col_count + masked(column, mask), rows]

    own = replica * col_count + column
    copies = {}

    def send(name, source, target, device):
        at = number[name]
        copies[name] = pltpu.make_async_remote_copy(
            src_ref=source, dst_ref=target, send_sem=send_sem.at[at], recv_sem=recv_sem.at[at],
            device_id=device, device_id_type=MESH,
        )
        copies[name].start()

    def spread(steps, half, mask, done):
        rows = pl.ds(half * half_rows, half_rows)
        source = in_ref.at[rows] if steps == 0 and mask == 0 else block(steps, mask, half)
        for stage in range(done, len(orders[half])):
            send((half, stage, steps, mask), source, block(steps, mask, half), (replica, flipped(column, orders[half][stage])))
        send(("core", half, steps, mask), source, block(steps, mask, half), (replica, flipped(column, 0)))

    for steps in range(1, rep_count):
        send(("rep", steps), in_ref, out_ref.at[own], (lax.rem(replica + steps, rep_count), column))
    for half in range(2):
        spread(0, half, 0, 0)
    mine = pltpu.make_async_copy(in_ref, out_ref.at[own], local_sem)
    mine.start()

    def arrivals(stage, steps):
        for half in range(2):
            bit = orders[half][stage]
            for mask in submasks(orders[half][:stage]):
                copies[(half, stage, steps, mask)].wait_recv()
                spread(steps, half, mask | 1 << bit, stage + 1)

    stages = len(orders[0])
    for turn in range(rep_count + stages):
        if 0 < turn < rep_count:
            copies[("rep", turn)].wait_recv()
            for half in range(2):
                spread(turn, half, 0, 0)
        for stage in range(stages):
            if 0 <= turn - stage < rep_count:
                arrivals(stage, turn - stage)
    mine.wait()
    for name, copy in copies.items():
        if name[0] == "core":
            copy.wait_recv()
        copy.wait_send()


def gather_all(rows, rep_count, col_count, collective_id):
    _, number = gather_plan(rep_count, col_count.bit_length() - 1)
    blocks = rep_count * col_count
    size = rows.size * 2
    out = pl.pallas_call(
        functools.partial(gather_kernel, rep_count, col_count),
        out_shape=jax.ShapeDtypeStruct((blocks,) + rows.shape, rows.dtype),
        in_specs=[pl.BlockSpec(memory_space=pltpu.VMEM)],
        out_specs=pl.BlockSpec(memory_space=pltpu.VMEM),
        scratch_shapes=[
            pltpu.SemaphoreType.DMA((len(number),)),
            pltpu.SemaphoreType.DMA((len(number),)),
            pltpu.SemaphoreType.DMA,
        ],
        compiler_params=pltpu.CompilerParams(
            collective_id=collective_id, has_side_effects=True, vmem_limit_bytes=size * (blocks + 2) + (2 << 20)
        ),
    )(rows)
    return out.reshape(blocks * rows.shape[0], rows.shape[1])


def scatter_plan(rep_count, bit_count):
    outer = list(range(1, bit_count))
    orders = (outer[::-1], outer)
    shifts = list(range(1, rep_count)) + [0]
    masks = sorted(submasks(outer), key=lambda mask: -bin(mask).count("1"))
    names = [("core", steps, mask) for steps in shifts for mask in masks]
    for half in range(2):
        for stage in range(len(outer)):
            for steps in shifts:
                names += [(half, stage, steps, mask) for mask in submasks(orders[half][stage + 1 :])]
        names += [("rep", half, steps) for steps in range(1, rep_count)]
    return orders, shifts, masks, {name: at for at, name in enumerate(names)}


def scatter_kernel(rep_count, col_count, in_ref, out_ref, core_buf, *rest):
    bit_count = col_count.bit_length() - 1
    stages = bit_count - 1
    stage_bufs, (rep_buf, send_sem, recv_sem) = rest[:stages], rest[stages:]
    replica, column = lax.axis_index("rep"), lax.axis_index("ep")
    orders, shifts, masks, number = scatter_plan(rep_count, bit_count)
    half_rows = in_ref.shape[1] // 2
    greet(rep_count, bit_count, replica, column)
    copies = {}

    def send(name, source, target, device):
        at = number[name]
        copies[name] = pltpu.make_async_remote_copy(
            src_ref=source, dst_ref=target, send_sem=send_sem.at[at], recv_sem=recv_sem.at[at],
            device_id=device, device_id_type=MESH,
        )
        copies[name].start()

    def bound_for(steps, col):
        return lax.rem(replica + steps, rep_count) * col_count + col

    def core_slot(steps, mask):
        return core_buf.at[steps * len(masks) + masks.index(mask)]

    def stage_slot(half, stage, steps, mask):
        left = submasks(orders[half][stage + 1 :])
        return stage_bufs[stage].at[(half * rep_count + steps) * len(left) + left.index(mask)]

    def held(half, stage, steps, mask):
        if stage == 0:
            return core_slot(steps, mask).at[pl.ds(half * half_rows, half_rows)]
        return stage_slot(half, stage - 1, steps, mask)

    for steps in shifts:
        for mask in masks:
            other = flipped(column, 0)
            send(("core", steps, mask), in_ref.at[bound_for(steps, masked(other, mask))], core_slot(steps, mask), (replica, other))

    def onward(half, stage, steps):
        if stage == stages:
            if steps:
                send(("rep", half, steps), held(half, stage, steps, 0), rep_buf.at[half * rep_count + steps], (lax.rem(replica + steps, rep_count), column))
            return
        bit = orders[half][stage]
        for mask in submasks(orders[half][stage + 1 :]):
            send((half, stage, steps, mask), held(half, stage, steps, mask | 1 << bit), stage_slot(half, stage, steps, mask), (replica, flipped(column, bit)))

    def take_core(steps):
        for mask in masks:
            copies[("core", steps, mask)].wait_recv()
            slot = core_slot(steps, mask)
            slot[...] = slot[...] + in_ref[bound_for(steps, masked(column, mask))]
        for half in range(2):
            onward(half, 0, steps)

    def take_stage(stage, steps):
        for half in range(2):
            for mask in submasks(orders[half][stage + 1 :]):
                copies[(half, stage, steps, mask)].wait_recv()
                slot = stage_slot(half, stage, steps, mask)
                slot[...] = slot[...] + held(half, stage, steps, mask)[...]
            onward(half, stage + 1, steps)

    for turn in range(rep_count + stages):
        if turn < rep_count:
            take_core(shifts[turn])
        for stage in range(stages):
            if 0 <= turn - stage - 1 < rep_count:
                take_stage(stage, shifts[turn - stage - 1])
    for half in range(2):
        total = held(half, stages, 0, 0)[...].astype(jnp.float32)
        for steps in range(1, rep_count):
            copies[("rep", half, steps)].wait_recv()
            total = total + rep_buf[half * rep_count + steps].astype(jnp.float32)
        out_ref[pl.ds(half * half_rows, half_rows)] = total.astype(out_ref.dtype)
    for copy in copies.values():
        copy.wait_send()


def scatter_sum(partial, rep_count, col_count, out_dtype, collective_id):
    bit_count = col_count.bit_length() - 1
    orders, shifts, masks, number = scatter_plan(rep_count, bit_count)
    blocks = rep_count * col_count
    rows, width = partial.shape[0] // blocks, partial.shape[1]
    half = rows // 2
    buffers = [pltpu.VMEM((rep_count * len(masks), rows, width), partial.dtype)]
    for stage in range(bit_count - 1):
        buffers.append(pltpu.VMEM((2 * rep_count * len(masks) >> stage + 1, half, width), partial.dtype))
    buffers.append(pltpu.VMEM((2 * rep_count, half, width), partial.dtype))
    size = rows * width * 2
    return pl.pallas_call(
        functools.partial(scatter_kernel, rep_count, col_count),
        out_shape=jax.ShapeDtypeStruct((rows, width), out_dtype),
        in_specs=[pl.BlockSpec(memory_space=pltpu.VMEM)],
        out_specs=pl.BlockSpec(memory_space=pltpu.VMEM),
        scratch_shapes=buffers
        + [pltpu.SemaphoreType.DMA((len(number),)), pltpu.SemaphoreType.DMA((len(number),))],
        compiler_params=pltpu.CompilerParams(
            collective_id=collective_id,
            has_side_effects=True,
            vmem_limit_bytes=size * (2 * blocks + rep_count + 4) + (2 << 20),
        ),
    )(partial.reshape(blocks, rows, width))


def attend_kernel(col_count, table_ref, length_ref, pages_ref, query_ref, out_ref, keys, held, send_sem, recv_sem, local_sem):
    request_count, row_count, _ = query_ref.shape
    replica, column = lax.axis_index("rep"), lax.axis_index("ep")
    block_rows = row_count // col_count
    heads_dev = block_rows // SPEC
    barrier = pltpu.get_barrier_semaphore()
    for steps in range(1, col_count):
        pl.semaphore_signal(barrier, inc=1, device_id=(replica, lax.rem(column + steps, col_count)), device_id_type=MESH)
    pl.semaphore_wait(barrier, col_count - 1)

    def copy_of(request, steps):
        there = lax.rem(column + steps, col_count)
        return pltpu.make_async_remote_copy(
            src_ref=held.at[request, there], dst_ref=out_ref.at[column, request],
            send_sem=send_sem.at[request, steps], recv_sem=recv_sem.at[request, steps],
            device_id=(replica, there), device_id_type=MESH,
        )

    def own_copy(request):
        return pltpu.make_async_copy(held.at[request, column], out_ref.at[column, request], local_sem.at[request])

    def step(request, carry):
        for page in range(MAXP):
            keys[pl.ds(page * PAGE, PAGE), :] = pages_ref[table_ref[request, page]]
        scores = lax.dot_general(
            query_ref[request], keys[...], (((1,), (1,)), ((), ())), preferred_element_type=jnp.float32
        )
        position = lax.broadcasted_iota(jnp.int32, scores.shape, 1)
        offset = lax.broadcasted_iota(jnp.int32, (row_count, 1), 0) % block_rows // heads_dev
        scores = jnp.where(position < length_ref[request] - SPEC + 1 + offset, scores, -1e30)
        exponent = jnp.exp((scores - jnp.max(scores, axis=1, keepdims=True)) * SCORE_SCALE)
        probability = (exponent * (1.0 / jnp.sum(exponent, axis=1, keepdims=True))).astype(jnp.bfloat16)
        latent = jnp.dot(probability, keys[:, :LAT], preferred_element_type=jnp.float32)
        held[request] = latent.astype(jnp.bfloat16).reshape(col_count, block_rows, LAT)
        for steps in range(1, col_count):
            copy_of(request, steps).start()
        own_copy(request).start()
        return carry

    lax.fori_loop(0, request_count, step, 0)

    def finish(request, carry):
        for steps in range(1, col_count):
            copy_of(request, steps).wait()
        own_copy(request).wait()
        return carry

    lax.fori_loop(0, request_count, finish, 0)


def attend(pages, queries, table, lengths, col_count, collective_id):
    request_count = queries.shape[0]
    heads_dev = HEADS // col_count
    block_rows = SPEC * heads_dev
    query_rows = queries.reshape(request_count, SPEC, col_count, heads_dev, KVW)
    query_rows = query_rows.transpose(0, 2, 1, 3, 4).reshape(request_count, SPEC * HEADS, KVW)
    return pl.pallas_call(
        functools.partial(attend_kernel, col_count),
        out_shape=jax.ShapeDtypeStruct((col_count, request_count, block_rows, LAT), jnp.bfloat16),
        in_specs=[pl.BlockSpec(memory_space=pltpu.SMEM)] * 2 + [pl.BlockSpec(memory_space=pltpu.VMEM)] * 2,
        out_specs=pl.BlockSpec(memory_space=pltpu.VMEM),
        scratch_shapes=[
            pltpu.VMEM((MAXP * PAGE, KVW), jnp.bfloat16),
            pltpu.VMEM((request_count, col_count, block_rows, LAT), jnp.bfloat16),
            pltpu.SemaphoreType.DMA((request_count, col_count)),
            pltpu.SemaphoreType.DMA((request_count, col_count)),
            pltpu.SemaphoreType.DMA((request_count,)),
        ],
        compiler_params=pltpu.CompilerParams(
            collective_id=collective_id, has_side_effects=True, vmem_limit_bytes=32 << 20
        ),
    )(table, lengths, pages, query_rows)


def swap_kernel(rep_count, in_ref, out_ref, send_sem, recv_sem):
    replica, column = lax.axis_index("rep"), lax.axis_index("ep")
    greet(rep_count, 0, replica, column)
    copies = []
    for steps in range(1, rep_count):
        copies.append(
            pltpu.make_async_remote_copy(
                src_ref=in_ref, dst_ref=out_ref.at[steps - 1],
                send_sem=send_sem.at[steps], recv_sem=recv_sem.at[steps],
                device_id=(lax.rem(replica + steps, rep_count), column), device_id_type=MESH,
            )
        )
        copies[-1].start()
    for copy in copies:
        copy.wait()


def swap(rows, rep_count, collective_id):
    return pl.pallas_call(
        functools.partial(swap_kernel, rep_count),
        out_shape=jax.ShapeDtypeStruct((rep_count - 1,) + rows.shape, rows.dtype),
        in_specs=[pl.BlockSpec(memory_space=pltpu.VMEM)],
        out_specs=pl.BlockSpec(memory_space=pltpu.VMEM),
        scratch_shapes=[pltpu.SemaphoreType.DMA((rep_count,)), pltpu.SemaphoreType.DMA((rep_count,))],
        compiler_params=pltpu.CompilerParams(
            collective_id=collective_id, has_side_effects=True, vmem_limit_bytes=8 << 20
        ),
    )(rows)


def served_rows(own_rows, own_sheds, shifts):
    rep_count = lax.axis_size("rep")
    hits = own_sheds[:, None] == jnp.arange(REQ_DEV, dtype=jnp.int32)[None, :]
    leaving = [jnp.sum(jnp.where(hits[k][:, None], own_rows, 0), axis=0, keepdims=True) for k in range(own_sheds.shape[0])]
    leaving = jnp.concatenate(leaving, axis=0)
    arrived = leaving
    for steps in range(1, rep_count):
        moved = shifted(leaving, "rep", steps)
        arrived = jnp.where((shifts == steps)[:, None], moved, arrived)
    served = own_rows
    for k in range(own_sheds.shape[0]):
        served = jnp.where(hits[k][:, None], arrived[k][None, :], served)
    return served


def served_tokens(own_tokens, own_sheds, shifts, collective_id):
    rep_count = lax.axis_size("rep")
    owner = jnp.arange(own_tokens.shape[0], dtype=jnp.int32) // SPEC
    hits = own_sheds[:, None] == owner[None, :]
    width = own_tokens.shape[1]
    blocks = own_tokens.reshape(REQ_DEV, SPEC, width)
    shed = own_sheds.shape[0]
    block_hits = own_sheds[:, None] == jnp.arange(REQ_DEV, dtype=jnp.int32)[None, :]
    leaving = jnp.sum(jnp.where(block_hits[:, :, None, None], blocks[None], 0), axis=1)
    moved = swap(leaving.reshape(shed * SPEC, width), rep_count, collective_id)
    moved = moved.reshape(rep_count - 1, shed, SPEC, width)
    arrived = moved[0]
    for steps in range(2, rep_count):
        arrived = jnp.where((shifts == steps)[:, None, None], moved[steps - 1], arrived)
    served = own_tokens
    for k in range(shed):
        repeated = jnp.tile(arrived[k], (REQ_DEV, 1))
        served = jnp.where(hits[k][:, None], repeated, served)
    return served


def gate_columns(expert_ids, gate_weight, expert_home, device_count):
    target = jnp.sum(
        jnp.where(
            expert_ids[:, :, None] == jnp.arange(device_count, dtype=jnp.int32)[None, None, :],
            expert_home[None, None, :],
            0,
        ),
        axis=2,
    )
    return jnp.sum(
        jnp.where(
            target[:, :, None] == jnp.arange(device_count, dtype=jnp.int32)[None, None, :],
            gate_weight[:, :, None],
            0.0,
        ),
        axis=1,
    )


def per_device(
    latent_pages,
    queries,
    residual,
    page_count,
    last_fill,
    page_order,
    shed_slots,
    shed_shift,
    expert_ids,
    gate_weight,
    expert_home,
    norm_gain,
    value_up,
    out_weight,
    expert_in,
    expert_out,
):
    rep_count = lax.axis_size("rep")
    col_count = lax.axis_size("ep")
    device_count = rep_count * col_count
    replica = lax.axis_index("rep")
    me = replica * col_count + lax.axis_index("ep")
    own_counts = page_count[replica, 0, :]
    own_lengths = (own_counts - 1) * PAGE + last_fill[replica, 0, :]
    own_sheds = shed_slots[replica, 0, :]
    shifts = shed_shift[0]
    served_residual = served_rows(residual, own_sheds, shifts)
    gates = gate_columns(expert_ids, gate_weight, expert_home, device_count)
    gates_high = gates.astype(jnp.bfloat16)
    gates_low = (gates - gates_high.astype(jnp.float32)).astype(jnp.bfloat16)

    offsets = jnp.cumsum(own_counts) - own_counts
    page_steps = jnp.arange(MAXP, dtype=jnp.int32)
    positions = jnp.minimum(offsets[:, None] + page_steps[None, :], PAGES_DEV - 1)
    pages = latent_pages.reshape(PAGES_DEV, PAGE, KVW)
    table = page_order[0][positions]
    tokens_dev = REQ_DEV * SPEC
    heads_dev = value_up.shape[0]
    regrouped = attend(pages, queries, table, own_lengths, col_count, 3)
    row_block = regrouped.reshape(tokens_dev * col_count, heads_dev, LAT)
    lifted = jnp.einsum(
        "thl,hlv->thv", row_block, value_up, preferred_element_type=jnp.float32
    ).astype(jnp.bfloat16)
    own_branch = scatter_sum(
        jnp.dot(
            lifted.reshape(tokens_dev * col_count, heads_dev * VHEAD),
            out_weight,
            preferred_element_type=jnp.float32,
        ).astype(jnp.bfloat16),
        1,
        col_count,
        jnp.bfloat16,
        0,
    )
    served_branch = served_tokens(own_branch, own_sheds, shifts, 4)
    attn_proj = served_branch.reshape(REQ_DEV, SPEC * D)
    branch = served_branch.astype(jnp.float32)
    mixed = served_residual.reshape(tokens_dev, D).astype(jnp.float32) + branch
    square = jnp.mean(mixed * mixed, axis=1, keepdims=True)
    normed = (mixed * lax.rsqrt(square + NORM_EPS) * norm_gain).astype(jnp.bfloat16)
    spare = -2 * device_count % 128
    packed = jnp.concatenate(
        (normed, gates_high, gates_low, jnp.zeros((tokens_dev, spare), jnp.bfloat16)), axis=1
    )
    everyone = gather_all(packed, rep_count, col_count, 1)
    all_gates = everyone[:, D : D + 2 * device_count].astype(jnp.float32)
    picks = jnp.arange(2 * device_count, dtype=jnp.int32) % device_count == me
    gate = jnp.sum(jnp.where(picks[None, :], all_gates, 0.0), axis=1, keepdims=True)
    inner_act = jax.nn.silu(
        jnp.dot(everyone[:, :D], expert_in[0], preferred_element_type=jnp.float32)
    ).astype(jnp.bfloat16)
    outer_out = jnp.dot(inner_act, expert_out[0], preferred_element_type=jnp.float32)
    moe_sum = scatter_sum(
        (gate * outer_out).astype(jnp.bfloat16), rep_count, col_count, jnp.float32, 2
    )
    layer_out = (mixed + moe_sum).astype(jnp.bfloat16).reshape(REQ_DEV, SPEC * D)
    return (attn_proj, layer_out)


def solution(mesh):
    placed = (
        P(("rep", "ep"), None),
        P(("rep", "ep"), None),
        P(("rep", "ep"), None),
        P(None, "ep", None),
        P(None, "ep", None),
        P(("rep", "ep"), None),
        P(None, "ep", None),
        P("ep", None),
        P(("rep", "ep"), None),
        P(("rep", "ep"), None),
        P(),
        P(),
        P("ep", None, None),
        P("ep", None),
        P(("rep", "ep"), None, None),
        P(("rep", "ep"), None, None),
    )
    return jax.shard_map(
        per_device,
        mesh=mesh,
        in_specs=placed,
        out_specs=(P(("rep", "ep"), None), P(("rep", "ep"), None)),
        check_vma=False,
    )
```

profile of v0, /device:TPU:0, one launch (start us, length us, event | category | flops | bytes accessed | tf_op | source)
XLA Modules:
  0.0 206.4 jit_solution(16316795017623268894)
XLA Ops:
  0.7 1.0 dynamic-slice_reduce_fusion
  1.6 0.1 iota_compare_fusion.2
  1.7 1.5 select_reduce_fusion.3
  3.2 0.8 pad_maximum_fusion
  4.0 5.1 %collective-permute-start = (bf16[2,14336]{1,0:T(2,128)(2,1)}, bf16[2,14336]{1,0:T(2,128)(2,1)}, u32[]{:S(2)}, u32[]{:S(2)}) collective-permute-start(bf16[2,14336]{1,0:T(2,128)(2,1)} %pad_maximum_fusion), channel_id=1, source_target_pairs={{0,24},{8,0},{16,8},{24,16},{1,25},{9,1},{17,9},{25,17},{2,26},{10... | collective-permute-start | bytes 172040 | tf_op jit(solution)/shard_map/ppermute | solution.py:31
  9.1 1.0 collective-permute-start.2
  10.1 0.7 fusion.17
  10.8 0.2 reduce-window.8
  10.9 0.7 fusion.14
  11.6 0.1 compare_select_fusion
  11.7 0.1 reshape.260
  11.8 1.6 gather_fusion
  13.4 0.1 reshape.259.table_ref
  13.4 2.7 %reshape.270 = bf16[1179648]{0:T(1024)(128)(2,1)S(1)} reshape(bf16[8,147456]{1,0:T(8,128)(2,1)} %param.17) | data formatting | bytes 4718592
  16.2 3.6 %reshape.247 = bf16[8,4,8,8,576]{4,3,2,1,0:T(8,128)(2,1)} reshape(bf16[1179648]{0:T(1024)(128)(2,1)S(1)} %reshape.270) | data formatting | bytes 4718592 | tf_op jit(solution)/shard_map/reshape | solution.py:329
  19.7 3.5 %copy.28 = bf16[8,4,8,8,576]{4,3,1,2,0:T(8,128)(2,1)} copy(bf16[8,4,8,8,576]{4,3,2,1,0:T(8,128)(2,1)} %reshape.247) | data formatting | bytes 4718592 | tf_op jit(solution)/shard_map/reshape | solution.py:329
  23.3 7.8 %reshape.246.pages_ref = bf16[48,64,576]{2,1,0:T(8,128)(2,1)} reshape(bf16[48,36864]{1,0:T(8,128)(2,1)} %param.16) | data formatting | bytes 7077888 | tf_op jit(solution)/shard_map/reshape | solution.py:469
  31.0 2.1 %copy-done.2 = bf16[48,64,576]{2,1,0:T(8,128)(2,1)S(1)} copy-done((bf16[48,64,576]{2,1,0:T(8,128)(2,1)S(1)}, bf16[48,64,576]{2,1,0:T(8,128)(2,1)}, u32[]{:S(2)}) %copy-start.2) | copy-done | bytes 3538968
  33.1 1.7 copy-done.3
  34.9 29.0 %shard_map.167 = bf16[8,8,32,512]{3,2,1,0:T(8,128)(2,1)S(1)} custom-call(s32[8,12]{1,0:T(8,128)S(1)} %reshape.259.table_ref, s32[8]{0:T(128)S(1)} %get-tuple-element.15.length_ref, bf16[48,64,576]{2,1,0:T(8,128)(2,1)S(1)} %copy-done.2, bf16[8,256,576]{2,1,0:T(8,128)(2,1)S(1)} %bitcast.58), custom_call_target="tpu_custom_call" | custom-call | tf_op jit(solution)/shard_map/pallas_call | solution.py:331
  63.9 0.9 fusion.10
  64.8 5.2 %convolution_convert_fusion = bf16[256,3584]{1,0:T(8,128)(2,1)S(1)} fusion(bf16[256,1024]{0,1:T(8,128)(2,1)S(1)} %bitcast.65, bf16[1024,3584]{1,0:T(8,128)(2,1)} %param.29), kind=kOutput, calls=%fused_computation.6 | convolution fusion | flops 1879965696 | bytes 9699328 | tf_op jit(solution)/shard_map/dot_general | solution.py:479
  70.0 15.4 %shard_map.168 = bf16[32,3584]{1,0:T(8,128)(2,1)S(1)} custom-call(bf16[8,32,3584]{2,1,0:T(8,128)(2,1)S(1)} %bitcast.62), custom_call_target="tpu_custom_call" | custom-call | tf_op jit(solution)/shard_map/pallas_call | solution.py:260
  85.6 0.3 select_reduce_fusion.1
  85.9 8.3 %shard_map.169 = bf16[3,8,3584]{2,1,0:T(8,128)(2,1)S(1)} custom-call(bf16[8,3584]{1,0:T(8,128)(2,1)S(1)} %reshape.252.in_ref), custom_call_target="tpu_custom_call" | custom-call | tf_op jit(solution)/shard_map/pallas_call | solution.py:367
  94.4 0.1 select_select_fusion.1
  94.5 0.1 tile.21
  94.6 0.1 tile.22
  94.6 0.1 tile.24
  94.8 0.1 broadcast_compare_fusion
  94.9 0.1 copy.32
  94.9 0.1 copy.33
  95.0 0.7 select_reduce_fusion.5
  95.7 0.1 select_reduce_fusion.4
  95.9 1.1 broadcast_select_fusion.2
  97.0 0.3 slice_reduce_fusion.1
  97.4 0.1 select_convert_fusion
  97.5 0.1 reshape.257
  97.6 0.3 multiply_reduce_fusion
  97.9 0.9 reshape.253
  98.8 0.1 multiply_convert_fusion.2
  99.0 0.1 concatenate.7.in_ref
  99.1 39.4 %shard_map.170 = bf16[32,32,3712]{2,1,0:T(8,128)(2,1)S(1)} custom-call(bf16[32,3712]{1,0:T(8,128)(2,1)S(1)} %concatenate.7.in_ref), custom_call_target="tpu_custom_call" | custom-call | tf_op jit(solution)/shard_map/pallas_call | solution.py:139
  138.5 10.7 %multiply_convert_fusion.1 = bf16[1024,1024]{1,0:T(8,128)(2,1)S(1)} fusion(bf16[1,3584,1024]{2,1,0:T(8,128)(2,1)} %param.30, bf16[1024,3712]{1,0:T(8,128)(2,1)S(1)} %bitcast.59), kind=kOutput, calls=%fused_computation.7 | convolution fusion | flops 7521435648 | bytes 16777216 | tf_op jit(solution)/shard_map/dot_general | solution.py:504
  149.2 0.1 select_reduce_fusion
  149.4 8.6 %multiply_convert_fusion = bf16[1024,3584]{1,0:T(8,128)(2,1)S(1)} fusion(bf16[1024,1024]{1,0:T(8,128)(2,1)S(1)} %multiply_convert_fusion.1, bf16[1,1024,3584]{2,1,0:T(8,128)(2,1)S(1)} %bitcast.67, f32[1024]{0:T(1024)S(1)} %select_reduce_fusion), kind=kOutput, calls=%fused_computation.1 | convolution fusion | flops 7523532800 | bytes 16781312 | tf_op jit(solution)/shard_map/dot_general | solution.py:506
  158.1 47.3 %shard_map.171 = f32[32,3584]{1,0:T(8,128)S(1)} custom-call(bf16[32,32,3584]{2,1,0:T(8,128)(2,1)S(1)} %bitcast.61), custom_call_target="tpu_custom_call" | custom-call | tf_op jit(solution)/shard_map/pallas_call | solution.py:260
  205.5 0.9 reshape.256
  (48 shorter events, 0.5 us)
Async XLA Ops:
  0.6 63.3 %copy-start = (bf16[8,512,128]{2,1,0:T(8,128)(2,1)S(1)}, bf16[8,512,128]{2,1,0:T(8,128)(2,1)}, u32[]{:S(2)}) copy-start(bf16[8,512,128]{2,1,0:T(8,128)(2,1)} %param.28) | copy-start | bytes 3145732
  4.0 91.9 %collective-permute-start = (bf16[2,14336]{1,0:T(2,128)(2,1)}, bf16[2,14336]{1,0:T(2,128)(2,1)}, u32[]{:S(2)}, u32[]{:S(2)}) collective-permute-start(bf16[2,14336]{1,0:T(2,128)(2,1)} %pad_maximum_fusion), channel_id=1, source_target_pairs={{0,24},{8,0},{16,8},{24,16},{1,25},{9,1},{17,9},{25,17},{2,26},{10... | collective-permute-start | bytes 172040 | tf_op jit(solution)/shard_map/ppermute | solution.py:31
  9.1 86.8 %collective-permute-start.1 = (bf16[2,14336]{1,0:T(2,128)(2,1)}, bf16[2,14336]{1,0:T(2,128)(2,1)}, u32[]{:S(2)}, u32[]{:S(2)}) collective-permute-start(bf16[2,14336]{1,0:T(2,128)(2,1)} %pad_maximum_fusion), channel_id=1, source_target_pairs={{0,16},{8,24},{16,0},{24,8},{1,17},{9,25},{17,1},{25,9},{2,18},{10... | collective-permute-start | bytes 172040 | tf_op jit(solution)/shard_map/ppermute | solution.py:31
  9.1 86.8 %collective-permute-start.2 = (bf16[2,14336]{1,0:T(2,128)(2,1)}, bf16[2,14336]{1,0:T(2,128)(2,1)}, u32[]{:S(2)}, u32[]{:S(2)}) collective-permute-start(bf16[2,14336]{1,0:T(2,128)(2,1)} %pad_maximum_fusion), channel_id=1, source_target_pairs={{0,8},{8,16},{16,24},{24,0},{1,9},{9,17},{17,25},{25,1},{2,10},{10... | collective-permute-start | bytes 172040 | tf_op jit(solution)/shard_map/ppermute | solution.py:31
  31.0 2.1 %copy-start.2 = (bf16[48,64,576]{2,1,0:T(8,128)(2,1)S(1)}, bf16[48,64,576]{2,1,0:T(8,128)(2,1)}, u32[]{:S(2)}) copy-start(bf16[48,64,576]{2,1,0:T(8,128)(2,1)} %reshape.246.pages_ref) | copy-start | bytes 10616836
  33.1 1.7 copy-start.3
  70.0 24.4 %copy-start.9 = (s32[1,2]{1,0:T(1,128)S(1)}, s32[1,2]{1,0:T(1,128)}, u32[]{:S(2)}) copy-start(s32[1,2]{1,0:T(1,128)} %param.23) | copy-start | bytes 28
  70.0 24.9 %copy-start.6 = (s32[32,8]{0,1:T(8,128)S(1)}, s32[32,8]{0,1:T(8,128)}, u32[]{:S(2)}) copy-start(s32[32,8]{0,1:T(8,128)} %param.24) | copy-start | bytes 3076
  70.0 24.9 %copy-start.7 = (f32[32,8]{0,1:T(8,128)S(1)}, f32[32,8]{0,1:T(8,128)}, u32[]{:S(2)}) copy-start(f32[32,8]{0,1:T(8,128)} %param.25) | copy-start | bytes 3076
  70.0 25.0 %copy-start.8 = (s32[32]{0:T(128)S(1)}, s32[32]{0:T(128)}, u32[]{:S(2)}) copy-start(s32[32]{0:T(128)} %param.26) | copy-start | bytes 388
  70.0 27.3 %copy-start.4 = (bf16[8,14336]{1,0:T(8,128)(2,1)S(1)}, bf16[8,14336]{1,0:T(8,128)(2,1)}, u32[]{:S(2)}) copy-start(bf16[8,14336]{1,0:T(8,128)(2,1)} %param.18) | copy-start | bytes 688132
  85.5 13.4 %copy-start.5 = (f32[3584]{0:T(1024)S(1)}, f32[3584]{0:T(1024)}, u32[]{:S(2)}) copy-start(f32[3584]{0:T(1024)} %param.27) | copy-start | bytes 43012
  99.1 50.3 %slice-start = ((s8[7340032]{0:T(1024)(128)(4,1)}), s8[4194304]{0:T(1024)(128)(4,1)S(1)}, s32[]{:S(2)}) async-start(s8[7340032]{0:T(1024)(128)(4,1)} %bitcast.66), calls=%async_computation | async-start | bytes 8388608
  138.5 10.9 %slice-start.1 = ((s8[7340032]{0:T(1024)(128)(4,1)}), s8[3145728]{0:T(1024)(128)(4,1)S(1)}, s32[]{:S(2)}) async-start(s8[7340032]{0:T(1024)(128)(4,1)} %bitcast.66), calls=%async_computation.1 | async-start | bytes 6291456
  158.0 48.3 %copy-start.1 = (bf16[8,512,128]{2,1,0:T(8,128)(2,1)S(1)}, bf16[8,512,128]{2,1,0:T(8,128)(2,1)}, u32[]{:S(2)}) copy-start(bf16[8,512,128]{2,1,0:T(8,128)(2,1)} %param.28) | copy-start | bytes 3145732
where the time goes:
time: 207 us; the launch traced here: 206 us
  Pallas kernels  140 us (68%)
  local copies, waits for them, and re-layouts  27.9 us (13%)
  matrix products  25.4 us (12%)
  other arithmetic  6.43 us (3%)
  starting transfers between devices  6.09 us (3%)
    pallas_call x2, Pallas kernels, scatter_sum(): pl.pallas_call(functools.partial(scatter_kernel, rep_count, col_count), o...  62.7 us
    pallas_call x1, Pallas kernels, gather_all(): pl.pallas_call(functools.partial(gather_kernel, rep_count, col_count), ou...  39.4 us
    pallas_call x1, Pallas kernels, attend(): pl.pallas_call(functools.partial(attend_kernel, col_count), out_shape=jax...  29 us
    dot_general x1, matrix products, per_device(): jnp.dot(everyone[:, :D], expert_in[0], preferred_element_type=jnp.float32)  10.7 us
    dot_general x1, matrix products, per_device(): jnp.dot(inner_act, expert_out[0], preferred_element_type=jnp.float32)  8.65 us
    pallas_call x1, Pallas kernels, swap(): pl.pallas_call(functools.partial(swap_kernel, rep_count), out_shape=jax.S...  8.34 us
    reshape x1, local copies, waits for them, and re-layouts, per_device(): pages = latent_pages.reshape(PAGES_DEV, PAGE, KVW)  7.76 us
    reshape x2, local copies, waits for them, and re-layouts, attend(): query_rows = queries.reshape(request_count, SPEC, col_count, heads_dev, KVW)  7.07 us
  transfers between devices with their start and end apart: 3, of which 0 were waited for; matrix products, arithmetic and copies ran while one was open for 14% of the time, Pallas kernels for 26%

commit v1 on v0

--- a/solution.py
+++ b/solution.py
@@ -272,14 +272,67 @@
     )(partial.reshape(blocks, rows, width))
 
 
-def attend_kernel(col_count, table_ref, length_ref, pages_ref, query_ref, out_ref, keys, held, send_sem, recv_sem, local_sem):
-    request_count, row_count, _ = query_ref.shape
+PAIR = 2 * KVW // 128
+KEYW = -(-KVW // 128) * 128
+
+
+def split_pairs(flat, row, stride_rows, count):
+    tiles = [flat[pl.ds(stride_rows * j + row, count, stride=stride_rows * PAIR), :] for j in range(PAIR)]
+    low = lax.broadcasted_iota(jnp.int32, (count, 128), 1) < 64
+    half = PAIR // 2
+    turned = [pltpu.roll(tile, 64, 1) for tile in tiles[half:]]
+    even = tiles[:half] + [jnp.where(low, tiles[half], 0.0)]
+    odd = [jnp.where(low, turned[c], turned[c + 1]) for c in range(half)] + [jnp.where(low, turned[half], 0.0)]
+    return even, odd
+
+
+def widen(source, rows, flat, pairs):
+    def step(at, carry):
+        base = pl.multiple_of(at * PAIR * 128, 128)
+        block = source[rows, pl.ds(base, PAIR * 128)].astype(jnp.float32)
+        for j in range(PAIR):
+            flat[pl.ds(pl.multiple_of((at * PAIR + j) * 8, 8), 8), :] = block[:, j * 128 : (j + 1) * 128]
+        return carry
+
+    lax.fori_loop(0, pairs, step, 0, unroll=4)
+
+
+def attend_kernel(
+    col_count, count_ref, fill_ref, order_ref, pages_ref, query_ref, out_ref,
+    page_flat, query_flat, paged, keys, raw, order_mat, held, send_sem, recv_sem, local_sem,
+):
+    request_count = REQ_DEV
+    row_count = SPEC * HEADS
     replica, column = lax.axis_index("rep"), lax.axis_index("ep")
     block_rows = row_count // col_count
     heads_dev = block_rows // SPEC
     barrier = pltpu.get_barrier_semaphore()
     for steps in range(1, col_count):
         pl.semaphore_signal(barrier, inc=1, device_id=(replica, lax.rem(column + steps, col_count)), device_id_type=MESH)
+
+    row = lax.broadcasted_iota(jnp.int32, (row_count, row_count), 0)
+    place = lax.broadcasted_iota(jnp.int32, (row_count, row_count), 1)
+    head = row // block_rows * heads_dev + row % heads_dev
+    spot = row % block_rows // heads_dev
+    wanted = head % 2 * (row_count // 2) + (spot * HEADS + head) // 2
+    order_mat[...] = jnp.where(place == wanted, 1.0, 0.0).astype(jnp.bfloat16)
+
+    def group_step(group, carry):
+        widen(pages_ref, pl.ds(pl.multiple_of(group * 8, 8), 8), page_flat, PAGE // 2)
+
+        def page_step(page, carry):
+            even, odd = split_pairs(page_flat, page, 8, PAGE // 2)
+            for c in range(KEYW // 128):
+                lanes = pl.ds(c * 128, 128)
+                paged[group * 8 + page, pl.ds(0, PAGE // 2), lanes] = even[c].astype(jnp.bfloat16)
+                paged[group * 8 + page, pl.ds(PAGE // 2, PAGE // 2), lanes] = odd[c].astype(jnp.bfloat16)
+            return carry
+
+        lax.fori_loop(0, 8, page_step, 0)
+        return carry
+
+    lax.fori_loop(0, PAGES_DEV // 8, group_step, 0)
+    widen(query_ref, slice(None), query_flat, row_count // 2)
     pl.semaphore_wait(barrier, col_count - 1)
 
     def copy_of(request, steps):
@@ -293,15 +346,24 @@
     def own_copy(request):
         return pltpu.make_async_copy(held.at[request, column], out_ref.at[column, request], local_sem.at[request])
 
-    def step(request, carry):
+    def step(request, offset):
+        count = count_ref[replica, 0, request]
+        length = (count - 1) * PAGE + fill_ref[replica, 0, request]
         for page in range(MAXP):
-            keys[pl.ds(page * PAGE, PAGE), :] = pages_ref[table_ref[request, page]]
-        scores = lax.dot_general(
-            query_ref[request], keys[...], (((1,), (1,)), ((), ())), preferred_element_type=jnp.float32
-        )
-        position = lax.broadcasted_iota(jnp.int32, scores.shape, 1)
-        offset = lax.broadcasted_iota(jnp.int32, (row_count, 1), 0) % block_rows // heads_dev
-        scores = jnp.where(position < length_ref[request] - SPEC + 1 + offset, scores, -1e30)
+            at = order_ref[0, jnp.minimum(offset + page, PAGES_DEV - 1)]
+            keys[pl.ds(page * PAGE, PAGE), :] = paged[at]
+        even, odd = split_pairs(query_flat, request, 8, row_count // 2)
+        for c in range(KEYW // 128):
+            lanes = pl.ds(c * 128, 128)
+            raw[pl.ds(0, row_count // 2), lanes] = even[c].astype(jnp.bfloat16)
+            raw[pl.ds(row_count // 2, row_count // 2), lanes] = odd[c].astype(jnp.bfloat16)
+        query = jnp.dot(order_mat[...], raw[...], preferred_element_type=jnp.float32).astype(jnp.bfloat16)
+        scores = lax.dot_general(query, keys[...], (((1,), (1,)), ((), ())), preferred_element_type=jnp.float32)
+        entry = lax.broadcasted_iota(jnp.int32, (1, MAXP * PAGE), 1)
+        inside = entry % PAGE
+        position = entry - inside + inside % (PAGE // 2) * 2 + inside // (PAGE // 2)
+        spare = lax.broadcasted_iota(jnp.int32, (row_count, 1), 0) % block_rows // heads_dev
+        scores = jnp.where(position < length - SPEC + 1 + spare, scores, -1e30)
         exponent = jnp.exp((scores - jnp.max(scores, axis=1, keepdims=True)) * SCORE_SCALE)
         probability = (exponent * (1.0 / jnp.sum(exponent, axis=1, keepdims=True))).astype(jnp.bfloat16)
         latent = jnp.dot(probability, keys[:, :LAT], preferred_element_type=jnp.float32)
@@ -309,7 +371,7 @@
         for steps in range(1, col_count):
             copy_of(request, steps).start()
         own_copy(request).start()
-        return carry
+        return offset + count
 
     lax.fori_loop(0, request_count, step, 0)
 
@@ -322,28 +384,31 @@
     lax.fori_loop(0, request_count, finish, 0)
 
 
-def attend(pages, queries, table, lengths, col_count, collective_id):
+def attend(pages, queries, counts, fills, order, col_count, collective_id):
     request_count = queries.shape[0]
-    heads_dev = HEADS // col_count
-    block_rows = SPEC * heads_dev
-    query_rows = queries.reshape(request_count, SPEC, col_count, heads_dev, KVW)
-    query_rows = query_rows.transpose(0, 2, 1, 3, 4).reshape(request_count, SPEC * HEADS, KVW)
+    row_count = SPEC * HEADS
+    block_rows = row_count // col_count
     return pl.pallas_call(
         functools.partial(attend_kernel, col_count),
         out_shape=jax.ShapeDtypeStruct((col_count, request_count, block_rows, LAT), jnp.bfloat16),
-        in_specs=[pl.BlockSpec(memory_space=pltpu.SMEM)] * 2 + [pl.BlockSpec(memory_space=pltpu.VMEM)] * 2,
+        in_specs=[pl.BlockSpec(memory_space=pltpu.SMEM)] * 3 + [pl.BlockSpec(memory_space=pltpu.VMEM)] * 2,
         out_specs=pl.BlockSpec(memory_space=pltpu.VMEM),
         scratch_shapes=[
-            pltpu.VMEM((MAXP * PAGE, KVW), jnp.bfloat16),
+            pltpu.VMEM((8 * PAGE * KVW // 128, 128), jnp.float32),
+            pltpu.VMEM((8 * row_count * KVW // 128, 128), jnp.float32),
+            pltpu.VMEM((PAGES_DEV, PAGE, KEYW), jnp.bfloat16),
+            pltpu.VMEM((MAXP * PAGE, KEYW), jnp.bfloat16),
+            pltpu.VMEM((row_count, KEYW), jnp.bfloat16),
+            pltpu.VMEM((row_count, row_count), jnp.bfloat16),
             pltpu.VMEM((request_count, col_count, block_rows, LAT), jnp.bfloat16),
             pltpu.SemaphoreType.DMA((request_count, col_count)),
             pltpu.SemaphoreType.DMA((request_count, col_count)),
             pltpu.SemaphoreType.DMA((request_count,)),
         ],
         compiler_params=pltpu.CompilerParams(
-            collective_id=collective_id, has_side_effects=True, vmem_limit_bytes=32 << 20
+            collective_id=collective_id, has_side_effects=True, vmem_limit_bytes=36 << 20
         ),
-    )(table, lengths, pages, query_rows)
+    )(counts, fills, order, pages, queries)
 
 
 def swap_kernel(rep_count, in_ref, out_ref, send_sem, recv_sem):
@@ -454,8 +519,6 @@
     device_count = rep_count * col_count
     replica = lax.axis_index("rep")
     me = replica * col_count + lax.axis_index("ep")
-    own_counts = page_count[replica, 0, :]
-    own_lengths = (own_counts - 1) * PAGE + last_fill[replica, 0, :]
     own_sheds = shed_slots[replica, 0, :]
     shifts = shed_shift[0]
     served_residual = served_rows(residual, own_sheds, shifts)
@@ -463,14 +526,9 @@
     gates_high = gates.astype(jnp.bfloat16)
     gates_low = (gates - gates_high.astype(jnp.float32)).astype(jnp.bfloat16)
 
-    offsets = jnp.cumsum(own_counts) - own_counts
-    page_steps = jnp.arange(MAXP, dtype=jnp.int32)
-    positions = jnp.minimum(offsets[:, None] + page_steps[None, :], PAGES_DEV - 1)
-    pages = latent_pages.reshape(PAGES_DEV, PAGE, KVW)
-    table = page_order[0][positions]
     tokens_dev = REQ_DEV * SPEC
     heads_dev = value_up.shape[0]
-    regrouped = attend(pages, queries, table, own_lengths, col_count, 3)
+    regrouped = attend(latent_pages, queries, page_count, last_fill, page_order, col_count, 3)
     row_block = regrouped.reshape(tokens_dev * col_count, heads_dev, LAT)
     lifted = jnp.einsum(
         "thl,hlv->thv", row_block, value_up, preferred_element_type=jnp.float32

time: 207 us -> 188 us (0.908)
  local copies, waits for them, and re-layouts: 27.9 us -> 9.7 us
  Pallas kernels: 140 us -> 144 us
  matrix products: 25.4 us -> 22.1 us
    reshape x3 -> x0, local copies, waits for them, and re-layouts: 14.8 us -> none  [the longest x1 7.76 us: per_device(): pages = latent_pages.reshape(PAGES_DEV, PAGE, KVW)]
    pallas_call x1, Pallas kernels: 29 us -> 33.8 us  [attend(): pl.pallas_call(functools.partial(attend_kernel, col_count), out_shape=jax...]
    dot_general x1, matrix products: 5.17 us -> 2.09 us  [per_device(): jnp.dot(lifted.reshape(tokens_dev * col_count, heads_dev * VHEAD), out_we...]
    unnamed x27 -> x30, local copies, waits for them, and re-layouts: 6.81 us -> 5.89 us
  transfers between devices with their start and end apart: 3 -> 3, of which waited for: 0 -> 0; matrix products, arithmetic and copies ran while one was open for 14% -> 3% of each run, Pallas kernels for 26% -> 31%
where the time goes in v1:
time: 188 us
  Pallas kernels  144 us (77%)
  matrix products  22.1 us (12%)
  local copies, waits for them, and re-layouts  9.7 us (5%)
  starting transfers between devices  6.14 us (3%)
  other arithmetic  4.67 us (2%)
    pallas_call x2, Pallas kernels, scatter_sum(): pl.pallas_call(functools.partial(scatter_kernel, rep_count, col_count), o...  62.3 us
    pallas_call x1, Pallas kernels, gather_all(): pl.pallas_call(functools.partial(gather_kernel, rep_count, col_count), ou...  39.9 us
    pallas_call x1, Pallas kernels, attend(): pl.pallas_call(functools.partial(attend_kernel, col_count), out_shape=jax...  33.8 us
    dot_general x1, matrix products, per_device(): jnp.dot(everyone[:, :D], expert_in[0], preferred_element_type=jnp.float32)  10.7 us
    dot_general x1, matrix products, per_device(): jnp.dot(inner_act, expert_out[0], preferred_element_type=jnp.float32)  8.41 us
    pallas_call x1, Pallas kernels, swap(): pl.pallas_call(functools.partial(swap_kernel, rep_count), out_shape=jax.S...  8.37 us
    ppermute x3, starting transfers between devices, shifted(): return lax.ppermute(value, axis, pairs)  6.14 us
    unnamed x30, local copies, waits for them, and re-layouts  5.89 us
  transfers between devices with their start and end apart: 3, of which 0 were waited for; matrix products, arithmetic and copies ran while one was open for 3% of the time, Pallas kernels for 31%

profile of v1, /device:TPU:0, one launch (start us, length us, event | category | flops | bytes accessed | tf_op | source)
XLA Modules:
  0.0 188.0 jit_solution(16333605179804856425)
XLA Ops:
  0.6 0.0 copy-start
  0.7 1.0 dynamic-slice_reduce_fusion
  1.6 0.1 iota_compare_fusion.2
  1.7 1.5 select_reduce_fusion.3
  3.2 0.1 pad_maximum_fusion
  3.4 5.1 %collective-permute-start = (bf16[2,14336]{1,0:T(2,128)(2,1)S(1)}, bf16[2,14336]{1,0:T(2,128)(2,1)S(1)}, u32[]{:S(2)}, u32[]{:S(2)}) collective-permute-start(bf16[2,14336]{1,0:T(2,128)(2,1)S(1)} %pad_maximum_fusion), channel_id=1, source_target_pairs={{0,24},{8,0},{16,8},{24,16},{1,25},{9,1},{17,9},{25,17},{2,26},{10... | collective-permute-start | bytes 172040 | tf_op jit(solution)/shard_map/ppermute | solution.py:31
  8.5 1.0 collective-permute-start.2
  9.5 0.7 compare_bitcast_fusion
  10.2 2.0 %copy-done.1 = bf16[48,36864]{1,0:T(8,128)(2,1)S(1)} copy-done((bf16[48,36864]{1,0:T(8,128)(2,1)S(1)}, bf16[48,36864]{1,0:T(8,128)(2,1)}, u32[]{:S(2)}) %copy-start.1) | copy-done | bytes 3538968
  12.2 1.7 copy-done.2
  13.9 0.7 copy-done.3
  14.5 0.7 copy-done.4
  15.2 0.7 copy-done.5
  15.9 33.8 %shard_map.167 = bf16[8,8,32,512]{3,2,1,0:T(8,128)(2,1)S(1)} custom-call(s32[4,1,8]{2,1,0:T(1,128)S(1)} %copy-done.3, s32[4,1,8]{2,1,0:T(1,128)S(1)} %copy-done.4, s32[1,48]{1,0:T(1,128)S(1)} %copy-done.5, bf16[48,36864]{1,0:T(8,128)(2,1)S(1)} %copy-done.1, bf16[8,147456]{1,0:T(8,128)(2,1)S(1)} %copy-done.2), custom_call_target="tpu_custom_call" | custom-call | tf_op jit(solution)/shard_map/pallas_call | solution.py:391
  49.7 0.9 fusion.10
  50.6 0.0 copy-start.11
  50.6 0.0 copy-start.7
  50.6 2.1 %convolution_convert_fusion = bf16[256,3584]{1,0:T(8,128)(2,1)S(1)} fusion(bf16[256,1024]{0,1:T(8,128)(2,1)S(1)} %bitcast.42, bf16[1024,3584]{1,0:T(8,128)(2,1)S(1)} %copy-done.6), kind=kOutput, calls=%fused_computation.5 | convolution fusion | flops 1879965696 | bytes 9699328 | tf_op jit(solution)/shard_map/dot_general | solution.py:537
  52.7 15.2 %shard_map.168 = bf16[32,3584]{1,0:T(8,128)(2,1)S(1)} custom-call(bf16[8,32,3584]{2,1,0:T(8,128)(2,1)S(1)} %bitcast.40), custom_call_target="tpu_custom_call" | custom-call | tf_op jit(solution)/shard_map/pallas_call | solution.py:260
  67.9 0.1 broadcast_in_dim.182
  68.0 0.3 select_reduce_fusion.1
  68.4 8.4 %shard_map.169 = bf16[3,8,3584]{2,1,0:T(8,128)(2,1)S(1)} custom-call(bf16[8,3584]{1,0:T(8,128)(2,1)S(1)} %reshape.164.in_ref), custom_call_target="tpu_custom_call" | custom-call | tf_op jit(solution)/shard_map/pallas_call | solution.py:432
  76.8 0.1 select_select_fusion.1
  77.0 0.1 tile.21
  77.0 0.1 tile.22
  77.1 0.1 tile.24
  77.2 0.1 tile.25
  77.2 0.1 broadcast_compare_fusion
  77.3 0.1 copy.25
  77.4 0.1 copy.26
  77.5 0.7 select_reduce_fusion.5
  78.2 0.1 select_reduce_fusion.4
  78.4 0.2 broadcast_select_fusion.2
  78.7 0.3 slice_reduce_fusion.1
  79.0 0.1 select_convert_fusion
  79.1 0.1 reshape.169
  79.2 0.3 multiply_reduce_fusion
  79.5 0.9 reshape.165
  80.4 0.1 multiply_convert_fusion.2
  80.6 0.1 concatenate.7.in_ref
  80.7 39.9 %shard_map.170 = bf16[32,32,3712]{2,1,0:T(8,128)(2,1)S(1)} custom-call(bf16[32,3712]{1,0:T(8,128)(2,1)S(1)} %concatenate.7.in_ref), custom_call_target="tpu_custom_call" | custom-call | tf_op jit(solution)/shard_map/pallas_call | solution.py:139
  120.6 0.0 slice-start.1
  120.6 10.7 %multiply_convert_fusion.1 = bf16[1024,1024]{1,0:T(8,128)(2,1)S(1)} fusion(bf16[1,3584,1024]{2,1,0:T(8,128)(2,1)} %param.30, bf16[1024,3712]{1,0:T(8,128)(2,1)S(1)} %bitcast.37), kind=kOutput, calls=%fused_computation.6 | convolution fusion | flops 7521435648 | bytes 16777216 | tf_op jit(solution)/shard_map/dot_general | solution.py:562
  131.3 0.1 select_reduce_fusion
  131.5 8.4 %multiply_convert_fusion = bf16[1024,3584]{1,0:T(8,128)(2,1)S(1)} fusion(bf16[1024,1024]{1,0:T(8,128)(2,1)S(1)} %multiply_convert_fusion.1, bf16[1,1024,3584]{2,1,0:T(8,128)(2,1)S(1)} %bitcast.44, f32[1024]{0:T(1024)S(1)} %select_reduce_fusion), kind=kOutput, calls=%fused_computation | convolution fusion | flops 7523532800 | bytes 16781312 | tf_op jit(solution)/shard_map/dot_general | solution.py:564
  139.9 47.1 %shard_map.171 = f32[32,3584]{1,0:T(8,128)S(1)} custom-call(bf16[32,32,3584]{2,1,0:T(8,128)(2,1)S(1)} %bitcast.39), custom_call_target="tpu_custom_call" | custom-call | tf_op jit(solution)/shard_map/pallas_call | solution.py:260
  187.0 0.1 add_convert_fusion
  187.1 0.9 reshape.168
  (40 shorter events, 0.3 us)
Async XLA Ops:
  0.6 49.0 %copy-start = (bf16[8,512,128]{2,1,0:T(8,128)(2,1)S(1)}, bf16[8,512,128]{2,1,0:T(8,128)(2,1)}, u32[]{:S(2)}) copy-start(bf16[8,512,128]{2,1,0:T(8,128)(2,1)} %param.28) | copy-start | bytes 3145732
  3.4 75.0 %collective-permute-start = (bf16[2,14336]{1,0:T(2,128)(2,1)S(1)}, bf16[2,14336]{1,0:T(2,128)(2,1)S(1)}, u32[]{:S(2)}, u32[]{:S(2)}) collective-permute-start(bf16[2,14336]{1,0:T(2,128)(2,1)S(1)} %pad_maximum_fusion), channel_id=1, source_target_pairs={{0,24},{8,0},{16,8},{24,16},{1,25},{9,1},{17,9},{25,17},{2,26},{10... | collective-permute-start | bytes 172040 | tf_op jit(solution)/shard_map/ppermute | solution.py:31
  8.5 69.9 %collective-permute-start.1 = (bf16[2,14336]{1,0:T(2,128)(2,1)S(1)}, bf16[2,14336]{1,0:T(2,128)(2,1)S(1)}, u32[]{:S(2)}, u32[]{:S(2)}) collective-permute-start(bf16[2,14336]{1,0:T(2,128)(2,1)S(1)} %pad_maximum_fusion), channel_id=1, source_target_pairs={{0,16},{8,24},{16,0},{24,8},{1,17},{9,25},{17,1},{25,9},{2,18},{10... | collective-permute-start | bytes 172040 | tf_op jit(solution)/shard_map/ppermute | solution.py:31
  8.5 69.9 %collective-permute-start.2 = (bf16[2,14336]{1,0:T(2,128)(2,1)S(1)}, bf16[2,14336]{1,0:T(2,128)(2,1)S(1)}, u32[]{:S(2)}, u32[]{:S(2)}) collective-permute-start(bf16[2,14336]{1,0:T(2,128)(2,1)S(1)} %pad_maximum_fusion), channel_id=1, source_target_pairs={{0,8},{8,16},{16,24},{24,0},{1,9},{9,17},{17,25},{25,1},{2,10},{10... | collective-permute-start | bytes 172040 | tf_op jit(solution)/shard_map/ppermute | solution.py:31
  10.2 2.0 %copy-start.1 = (bf16[48,36864]{1,0:T(8,128)(2,1)S(1)}, bf16[48,36864]{1,0:T(8,128)(2,1)}, u32[]{:S(2)}) copy-start(bf16[48,36864]{1,0:T(8,128)(2,1)} %pages_ref.1) | copy-start | bytes 10616836
  12.2 1.7 copy-start.2
  13.9 0.7 copy-start.3
  14.5 0.7 copy-start.4
  15.2 0.7 copy-start.5
  15.9 34.7 %copy-start.6 = (bf16[1024,3584]{1,0:T(8,128)(2,1)S(1)}, bf16[1024,3584]{1,0:T(8,128)(2,1)}, u32[]{:S(2)}) copy-start(bf16[1024,3584]{1,0:T(8,128)(2,1)} %param.29) | copy-start | bytes 22020100
  50.6 26.8 %copy-start.9 = (s32[32,8]{0,1:T(8,128)S(1)}, s32[32,8]{0,1:T(8,128)}, u32[]{:S(2)}) copy-start(s32[32,8]{0,1:T(8,128)} %param.24) | copy-start | bytes 3076
  50.6 26.8 %copy-start.10 = (f32[32,8]{0,1:T(8,128)S(1)}, f32[32,8]{0,1:T(8,128)}, u32[]{:S(2)}) copy-start(f32[32,8]{0,1:T(8,128)} %param.25) | copy-start | bytes 3076
  50.6 26.9 %copy-start.11 = (s32[32]{0:T(128)S(1)}, s32[32]{0:T(128)}, u32[]{:S(2)}) copy-start(s32[32]{0:T(128)} %param.26) | copy-start | bytes 388
  50.6 28.4 %copy-start.7 = (bf16[8,14336]{1,0:T(8,128)(2,1)S(1)}, bf16[8,14336]{1,0:T(8,128)(2,1)}, u32[]{:S(2)}) copy-start(bf16[8,14336]{1,0:T(8,128)(2,1)} %param.18) | copy-start | bytes 688132
  52.7 27.7 %copy-start.8 = (f32[3584]{0:T(1024)S(1)}, f32[3584]{0:T(1024)}, u32[]{:S(2)}) copy-start(f32[3584]{0:T(1024)} %param.27) | copy-start | bytes 43012
  80.7 50.8 %slice-start = ((s8[7340032]{0:T(1024)(128)(4,1)}), s8[4194304]{0:T(1024)(128)(4,1)S(1)}, s32[]{:S(2)}) async-start(s8[7340032]{0:T(1024)(128)(4,1)} %bitcast.43), calls=%async_computation | async-start | bytes 8388608
  120.6 10.9 %slice-start.1 = ((s8[7340032]{0:T(1024)(128)(4,1)}), s8[3145728]{0:T(1024)(128)(4,1)S(1)}, s32[]{:S(2)}) async-start(s8[7340032]{0:T(1024)(128)(4,1)} %bitcast.43), calls=%async_computation.1 | async-start | bytes 6291456

commit v2 on v1

--- a/solution.py
+++ b/solution.py
@@ -441,6 +441,289 @@
     )(rows)
 
 
+LEAD = 1
+FIRST = 512
+SECOND = 512
+
+
+def moe_keys(bit_count):
+    outer = list(range(1, bit_count))
+    spread_orders = (outer, outer[::-1])
+    reduce_orders = (outer[::-1], outer)
+    masks = sorted(submasks(outer), key=lambda mask: -bin(mask).count("1"))
+    keys = [("spread", "rep", 0, 0)]
+    for half in range(2):
+        for stage in range(len(outer)):
+            keys += [("spread", half, stage, mask) for mask in submasks(spread_orders[half][:stage])]
+        keys += [("spread", "core", half, mask) for mask in masks]
+    keys += [("reduce", "core", 0, mask) for mask in masks]
+    for half in range(2):
+        for stage in range(len(outer)):
+            keys += [("reduce", half, stage, mask) for mask in submasks(reduce_orders[half][stage + 1 :])]
+        keys.append(("reduce", "rep", half, 0))
+    return spread_orders, reduce_orders, masks, {key: at for at, key in enumerate(keys)}
+
+
+def moe_kernel(
+    rep_count, col_count, in_ref, in_weight, out_weight, out_ref,
+    got, held_in, held_out, inner, gate, partial, core_buf, *rest,
+):
+    bit_count = col_count.bit_length() - 1
+    stages = bit_count - 1
+    stage_bufs, (rep_buf, send_sem, recv_sem, local_sem) = rest[:stages], rest[stages:]
+    replica, column = lax.axis_index("rep"), lax.axis_index("ep")
+    me = replica * col_count + column
+    device_count = rep_count * col_count
+    spread_orders, reduce_orders, masks, number = moe_keys(bit_count)
+    rows = in_ref.shape[0]
+    width = out_ref.shape[1]
+    half_rows = rows // 2
+    other = flipped(column, 0)
+    loads = [
+        pltpu.make_async_copy(in_weight.at[0], held_in, local_sem.at[1]),
+        pltpu.make_async_copy(out_weight.at[0], held_out, local_sem.at[2]),
+    ]
+    for load in loads:
+        load.start()
+    greet(rep_count, bit_count, replica, column)
+
+    def origin(steps):
+        return lax.rem(replica + rep_count - steps, rep_count)
+
+    def block(steps, mask, half):
+        return got.at[origin(steps) * col_count + masked(column, mask), pl.ds(half * half_rows, half_rows)]
+
+    def core_slot(steps, mask):
+        return core_buf.at[steps * len(masks) + masks.index(mask)]
+
+    def stage_slot(half, stage, steps, mask):
+        left = submasks(reduce_orders[half][stage + 1 :])
+        return stage_bufs[stage].at[(half * rep_count + steps) * len(left) + left.index(mask)]
+
+    def partly(half, stage, steps, mask):
+        if stage == 0:
+            return core_slot(steps, mask).at[pl.ds(half * half_rows, half_rows)]
+        return stage_slot(half, stage - 1, steps, mask)
+
+    def copy_of(key, steps, source=None):
+        way, kind, at, mask = key
+        if way == "spread":
+            if kind == "rep":
+                ends = in_ref, got.at[me], (lax.rem(replica + steps, rep_count), column)
+            elif kind == "core":
+                ends = block(steps, mask, at), block(steps, mask, at), (replica, other)
+            else:
+                there = (replica, flipped(column, spread_orders[kind][at]))
+                ends = block(steps, mask, kind), block(steps, mask, kind), there
+        elif kind == "core":
+            ends = partial.at[steps, masked(other, mask)], core_slot(steps, mask), (replica, other)
+        elif kind == "rep":
+            ends = partly(at, stages, steps, 0), rep_buf.at[at * rep_count + steps], (origin(steps), column)
+        else:
+            bit = reduce_orders[kind][at]
+            there = (replica, flipped(column, bit))
+            ends = partly(kind, at, steps, mask | 1 << bit), stage_slot(kind, at, steps, mask), there
+        slot = number[key] * rep_count + steps
+        return pltpu.make_async_remote_copy(
+            src_ref=ends[0] if source is None else source, dst_ref=ends[1],
+            send_sem=send_sem.at[slot], recv_sem=recv_sem.at[slot], device_id=ends[2], device_id_type=MESH,
+        )
+
+    def spread(steps, half, mask, done, source=None):
+        for stage in range(done, stages):
+            copy_of(("spread", half, stage, mask), steps, source).start()
+        copy_of(("spread", "core", half, mask), steps, source).start()
+
+    def take_rep(steps):
+        copy_of(("spread", "rep", 0, 0), steps).wait_recv()
+        for half in range(2):
+            spread(steps, half, 0, 0)
+
+    def take_spread(stage, steps):
+        for half in range(2):
+            bit = spread_orders[half][stage]
+            for mask in submasks(spread_orders[half][:stage]):
+                copy_of(("spread", half, stage, mask), steps).wait_recv()
+                spread(steps, half, mask | 1 << bit, stage + 1)
+
+    def take_all(steps):
+        for half in range(2):
+            for mask in masks:
+                copy_of(("spread", "core", half, mask), steps).wait_recv()
+
+    def onward(half, stage, steps):
+        if stage == stages:
+            @pl.when(steps != 0)
+            def _():
+                copy_of(("reduce", "rep", half, 0), steps).start()
+            return
+        for mask in submasks(reduce_orders[half][stage + 1 :]):
+            copy_of(("reduce", half, stage, mask), steps).start()
+
+    def take_core(steps):
+        for mask in masks:
+            copy_of(("reduce", "core", 0, mask), steps).wait_recv()
+            slot = core_slot(steps, mask)
+            slot[...] = slot[...] + partial[steps, masked(column, mask)]
+        for half in range(2):
+            onward(half, 0, steps)
+
+    def take_reduce(stage, steps):
+        for half in range(2):
+            for mask in submasks(reduce_orders[half][stage + 1 :]):
+                copy_of(("reduce", half, stage, mask), steps).wait_recv()
+                slot = stage_slot(half, stage, steps, mask)
+                slot[...] = slot[...] + partly(half, stage, steps, mask)[...]
+            onward(half, stage + 1, steps)
+
+    for steps in range(1, rep_count):
+        copy_of(("spread", "rep", 0, 0), steps).start()
+    for half in range(2):
+        spread(0, half, 0, 0, in_ref.at[pl.ds(half * half_rows, half_rows)])
+    mine = pltpu.make_async_copy(in_ref, got.at[me], local_sem.at[0])
+    mine.start()
+    for steps in range(LEAD + 1):
+        for stage in range(stages):
+            take_spread(stage, steps)
+            if stage == 0 and steps + 1 < rep_count:
+                take_rep(steps + 1)
+        if steps == 0:
+            mine.wait()
+            for load in loads:
+                load.wait()
+        take_all(steps)
+
+    tall = col_count * rows
+
+    def first(steps, chunk):
+        tokens = got[pl.ds(origin(steps) * col_count, col_count), :, pl.ds(0, width)].reshape(tall, width)
+        lanes = pl.ds(chunk * FIRST, FIRST)
+        hidden = jnp.dot(tokens, held_in[:, lanes], preferred_element_type=jnp.float32)
+        inner[:, lanes] = (hidden / (1.0 + jnp.exp(-hidden))).astype(jnp.bfloat16)
+
+    def weigh(steps):
+        spare = in_ref.shape[1] - width
+        listed = got[pl.ds(origin(steps) * col_count, col_count), :, pl.ds(width, spare)].reshape(tall, spare)
+        lane = lax.broadcasted_iota(jnp.int32, (tall, spare), 1)
+        mine = (lane % device_count == me) & (lane < 2 * device_count)
+        gate[...] = jnp.sum(jnp.where(mine, listed.astype(jnp.float32), 0.0), axis=1, keepdims=True)
+
+    def second(steps, chunk):
+        lanes = pl.ds(chunk * SECOND, SECOND)
+        outer = jnp.dot(inner[...], held_out[:, lanes], preferred_element_type=jnp.float32)
+        partial[steps, :, :, lanes] = (gate[...] * outer).astype(jnp.bfloat16).reshape(col_count, rows, SECOND)
+
+    first_count, second_count = inner.shape[1] // FIRST, width // SECOND
+
+    def grouped(phase):
+        return lax.rem(phase - 1 + LEAD, rep_count)
+
+    def phase_step(phase, carry):
+        now = grouped(phase)
+        last = grouped(phase - 1 + rep_count)
+        before = grouped(phase - 2 + rep_count)
+        coming = phase + LEAD
+
+        def when(condition, *calls):
+            @pl.when(condition)
+            def _():
+                for call in calls:
+                    call()
+
+        first(now, 0)
+        weigh(now)
+        when(phase > 1, lambda: take_core(last))
+        when(coming < rep_count, lambda: take_spread(0, coming))
+        for chunk in range(1, first_count):
+            first(now, chunk)
+        when(coming + 1 < rep_count, lambda: take_rep(coming + 1))
+        for chunk in range(second_count):
+            second(now, chunk)
+            if chunk == second_count // 4:
+                when(phase > 2, lambda: take_reduce(stages - 1, before))
+            if chunk == second_count // 2:
+                for stage in range(1, stages):
+                    when(coming < rep_count, functools.partial(take_spread, stage, coming))
+                for stage in range(stages - 1):
+                    when(phase > 1, functools.partial(take_reduce, stage, last))
+        for mask in masks:
+            copy_of(("reduce", "core", 0, mask), now).start()
+        when(coming < rep_count, lambda: take_all(coming))
+        return carry
+
+    lax.fori_loop(1, rep_count + 1, phase_step, 0)
+    take_core(grouped(rep_count))
+    take_reduce(stages - 1, grouped(rep_count - 1))
+    for stage in range(stages):
+        take_reduce(stage, grouped(rep_count))
+    for half in range(2):
+        total = partly(half, stages, 0, 0)[...].astype(jnp.float32)
+        for steps in range(1, rep_count):
+            copy_of(("reduce", "rep", half, 0), steps).wait_recv()
+            total = total + rep_buf[half * rep_count + steps].astype(jnp.float32)
+        out_ref[pl.ds(half * half_rows, half_rows)] = total
+
+    def settle(steps, carry):
+        for key in number:
+            if key[1] == "rep":
+                @pl.when(steps != 0)
+                def _():
+                    copy_of(key, steps).wait_send()
+            else:
+                copy_of(key, steps).wait_send()
+        return carry
+
+    lax.fori_loop(0, rep_count, settle, 0)
+
+
+def moe_bytes(rep_count, col_count, rows, packed, width, hidden):
+    blocks = rep_count * col_count
+    masks = col_count // 2
+    halves = rep_count * rows * width
+    stages = masks.bit_length() - 1
+    reduced = sum(halves * (masks >> stage + 1) for stage in range(stages))
+    tokens = blocks * rows * (packed + width) + halves * masks + reduced + halves
+    return 2 * (tokens + 2 * width * hidden + col_count * rows * hidden + rows * (packed + 2 * width))
+
+
+def moe_fused(rows, in_weight, out_weight, rep_count, col_count, collective_id):
+    bit_count = col_count.bit_length() - 1
+    _, _, masks, number = moe_keys(bit_count)
+    blocks = rep_count * col_count
+    count, packed = rows.shape
+    width, hidden = in_weight.shape[1:]
+    half = count // 2
+    stage_bufs = [
+        pltpu.VMEM((2 * rep_count * len(masks) >> stage + 1, half, width), jnp.bfloat16) for stage in range(bit_count - 1)
+    ]
+    slots = len(number) * rep_count
+    return pl.pallas_call(
+        functools.partial(moe_kernel, rep_count, col_count),
+        out_shape=jax.ShapeDtypeStruct((count, width), jnp.float32),
+        in_specs=[pl.BlockSpec(memory_space=pltpu.VMEM)] + [pl.BlockSpec(memory_space=pl.ANY)] * 2,
+        out_specs=pl.BlockSpec(memory_space=pltpu.VMEM),
+        scratch_shapes=[
+            pltpu.VMEM((blocks, count, packed), jnp.bfloat16),
+            pltpu.VMEM((width, hidden), jnp.bfloat16),
+            pltpu.VMEM((hidden, width), jnp.bfloat16),
+            pltpu.VMEM((col_count * count, hidden), jnp.bfloat16),
+            pltpu.VMEM((col_count * count, 1), jnp.float32),
+            pltpu.VMEM((rep_count, col_count, count, width), jnp.bfloat16),
+            pltpu.VMEM((rep_count * len(masks), count, width), jnp.bfloat16),
+        ]
+        + stage_bufs
+        + [
+            pltpu.VMEM((2 * rep_count, half, width), jnp.bfloat16),
+            pltpu.SemaphoreType.DMA((slots,)),
+            pltpu.SemaphoreType.DMA((slots,)),
+            pltpu.SemaphoreType.DMA((3,)),
+        ],
+        compiler_params=pltpu.CompilerParams(
+            collective_id=collective_id, has_side_effects=True, vmem_limit_bytes=56 << 20
+        ),
+    )(rows, in_weight, out_weight)
+
+
 def served_rows(own_rows, own_sheds, shifts):
     rep_count = lax.axis_size("rep")
     hits = own_sheds[:, None] == jnp.arange(REQ_DEV, dtype=jnp.int32)[None, :]
@@ -493,6 +776,21 @@
             0.0,
         ),
         axis=1,
+    )
+
+
+def moe_split(packed, expert_in, expert_out, me, rep_count, col_count):
+    device_count = rep_count * col_count
+    everyone = gather_all(packed, rep_count, col_count, 1)
+    all_gates = everyone[:, D : D + 2 * device_count].astype(jnp.float32)
+    picks = jnp.arange(2 * device_count, dtype=jnp.int32) % device_count == me
+    gate = jnp.sum(jnp.where(picks[None, :], all_gates, 0.0), axis=1, keepdims=True)
+    inner_act = jax.nn.silu(
+        jnp.dot(everyone[:, :D], expert_in[0], preferred_element_type=jnp.float32)
+    ).astype(jnp.bfloat16)
+    outer_out = jnp.dot(inner_act, expert_out[0], preferred_element_type=jnp.float32)
+    return scatter_sum(
+        (gate * outer_out).astype(jnp.bfloat16), rep_count, col_count, jnp.float32, 2
     )
 
 
@@ -554,17 +852,11 @@
     packed = jnp.concatenate(
         (normed, gates_high, gates_low, jnp.zeros((tokens_dev, spare), jnp.bfloat16)), axis=1
     )
-    everyone = gather_all(packed, rep_count, col_count, 1)
-    all_gates = everyone[:, D : D + 2 * device_count].astype(jnp.float32)
-    picks = jnp.arange(2 * device_count, dtype=jnp.int32) % device_count == me
-    gate = jnp.sum(jnp.where(picks[None, :], all_gates, 0.0), axis=1, keepdims=True)
-    inner_act = jax.nn.silu(
-        jnp.dot(everyone[:, :D], expert_in[0], preferred_element_type=jnp.float32)
-    ).astype(jnp.bfloat16)
-    outer_out = jnp.dot(inner_act, expert_out[0], preferred_element_type=jnp.float32)
-    moe_sum = scatter_sum(
-        (gate * outer_out).astype(jnp.bfloat16), rep_count, col_count, jnp.float32, 2
-    )
+    needed = moe_bytes(rep_count, col_count, tokens_dev, packed.shape[1], D, expert_in.shape[2])
+    if needed < 52 << 20:
+        moe_sum = moe_fused(packed, expert_in, expert_out, rep_count, col_count, 1)
+    else:
+        moe_sum = moe_split(packed, expert_in, expert_out, me, rep_count, col_count)
     layer_out = (mixed + moe_sum).astype(jnp.bfloat16).reshape(REQ_DEV, SPEC * D)
     return (attn_proj, layer_out)
 

time: 188 us -> 169 us (0.90)
  the two profiles are of different devices: /device:TPU:0 before, /device:TPU:16 now
where the time goes in v2:
time: 169 us
  Pallas kernels  145 us (86%)
  local copies, waits for them, and re-layouts  10.4 us (6%)
  other arithmetic  5.51 us (3%)
  starting transfers between devices  3.99 us (2%)
  matrix products  2.97 us (2%)
    pallas_call x1, Pallas kernels, moe_fused(): pl.pallas_call(functools.partial(moe_kernel, rep_count, col_count), out_s...  88.6 us
    pallas_call x1, Pallas kernels, attend(): pl.pallas_call(functools.partial(attend_kernel, col_count), out_shape=jax...  34.3 us
    pallas_call x1, Pallas kernels, scatter_sum(): pl.pallas_call(functools.partial(scatter_kernel, rep_count, col_count), o...  15.2 us
    pallas_call x1, Pallas kernels, swap(): pl.pallas_call(functools.partial(swap_kernel, rep_count), out_shape=jax.S...  7.04 us
    unnamed x26, local copies, waits for them, and re-layouts  5.88 us
    ppermute x3, starting transfers between devices, shifted(): return lax.ppermute(value, axis, pairs)  3.99 us
  transfers between devices with their start and end apart: 3, of which 0 were waited for; matrix products, arithmetic and copies ran while one was open for 3% of the time, Pallas kernels for 33%

profile of v2, /device:TPU:16, one launch (start us, length us, event | category | flops | bytes accessed | tf_op | source)
XLA Modules:
  0.0 168.9 jit_solution(9647075817659410757)
XLA Ops:
  0.6 0.0 copy-start
  0.6 1.0 dynamic-slice_reduce_fusion
  1.6 0.1 iota_compare_fusion.2
  1.7 1.5 select_reduce_fusion.2
  3.2 0.1 pad_maximum_fusion
  3.4 0.5 collective-permute-start
  3.9 3.5 %collective-permute-start.1 = (bf16[2,14336]{1,0:T(2,128)(2,1)S(1)}, bf16[2,14336]{1,0:T(2,128)(2,1)S(1)}, u32[]{:S(2)}, u32[]{:S(2)}) collective-permute-start(bf16[2,14336]{1,0:T(2,128)(2,1)S(1)} %pad_maximum_fusion), channel_id=1, source_target_pairs={{0,16},{8,24},{16,0},{24,8},{1,17},{9,25},{17,1},{25,9},{2,18},{10... | collective-permute-start | bytes 172040 | tf_op jit(solution)/shard_map/ppermute | solution.py:31
  7.4 0.0 collective-permute-start.2
  7.4 0.7 compare_bitcast_fusion
  8.0 2.0 %copy-done.1 = bf16[48,36864]{1,0:T(8,128)(2,1)S(1)} copy-done((bf16[48,36864]{1,0:T(8,128)(2,1)S(1)}, bf16[48,36864]{1,0:T(8,128)(2,1)}, u32[]{:S(2)}) %copy-start.1) | copy-done | bytes 3538968
  10.0 1.7 copy-done.2
  11.7 0.7 copy-done.3
  12.4 0.7 copy-done.4
  13.1 0.7 copy-done.5
  13.7 34.3 %shard_map.167 = bf16[8,8,32,512]{3,2,1,0:T(8,128)(2,1)S(1)} custom-call(s32[4,1,8]{2,1,0:T(1,128)S(1)} %copy-done.3, s32[4,1,8]{2,1,0:T(1,128)S(1)} %copy-done.4, s32[1,48]{1,0:T(1,128)S(1)} %copy-done.5, bf16[48,36864]{1,0:T(8,128)(2,1)S(1)} %copy-done.1, bf16[8,147456]{1,0:T(8,128)(2,1)S(1)} %copy-done.2), custom_call_target="tpu_custom_call" | custom-call | tf_op jit(solution)/shard_map/pallas_call | solution.py:391
  48.0 0.9 fusion.2
  48.9 2.1 %convolution_convert_fusion = bf16[256,3584]{1,0:T(8,128)(2,1)S(1)} fusion(bf16[256,1024]{0,1:T(8,128)(2,1)S(1)} %bitcast.28, bf16[1024,3584]{1,0:T(8,128)(2,1)S(1)} %copy-done.6), kind=kOutput, calls=%fused_computation | convolution fusion | flops 1879965696 | bytes 9699328 | tf_op jit(solution)/shard_map/dot_general | solution.py:835
  51.0 0.0 copy-start.9
  51.0 0.0 copy-start.10
  51.0 0.0 copy-start.11
  51.1 0.0 copy-start.7
  51.1 15.2 %shard_map.168 = bf16[32,3584]{1,0:T(8,128)(2,1)S(1)} custom-call(bf16[8,32,3584]{2,1,0:T(8,128)(2,1)S(1)} %bitcast.26), custom_call_target="tpu_custom_call" | custom-call | tf_op jit(solution)/shard_map/pallas_call | solution.py:260
  66.3 0.1 broadcast_in_dim.168
  66.4 0.3 select_reduce_fusion
  66.7 0.0 copy-start.8
  66.7 7.0 %shard_map.169 = bf16[3,8,3584]{2,1,0:T(8,128)(2,1)S(1)} custom-call(bf16[8,3584]{1,0:T(8,128)(2,1)S(1)} %reshape.147.in_ref), custom_call_target="tpu_custom_call" | custom-call | tf_op jit(solution)/shard_map/pallas_call | solution.py:432
  73.9 0.1 select_select_fusion.1
  74.0 0.1 broadcast_compare_fusion
  74.1 0.1 copy.25
  74.2 0.1 copy.26
  74.2 0.7 select_reduce_fusion.4
  74.9 0.1 select_reduce_fusion.3
  75.1 0.1 tile.21
  75.2 0.1 tile.22
  75.2 0.1 tile.24
  75.3 0.1 tile.25
  75.4 0.0 collective-permute-done.2
  75.4 0.2 broadcast_select_fusion.2
  75.7 0.3 slice_reduce_fusion.1
  76.0 0.1 select_convert_fusion
  76.1 0.1 reshape.150
  76.2 0.3 multiply_reduce_fusion
  76.5 0.9 reshape.148
  77.4 0.1 multiply_convert_fusion
  77.6 0.8 concatenate.7.in_ref
  78.4 88.6 %shard_map.170 = f32[32,3584]{1,0:T(8,128)} custom-call(bf16[32,3712]{1,0:T(8,128)(2,1)} %concatenate.7.in_ref, bf16[1,3584,1024]{2,1,0:T(8,128)(2,1)} %in_weight.1, bf16[1,1024,3584]{2,1,0:T(8,128)(2,1)} %out_weight.1), custom_call_target="tpu_custom_call" | custom-call | tf_op jit(solution)/shard_map/pallas_call | solution.py:700
  166.9 1.1 add_convert_fusion
  168.0 0.9 reshape.149
  (30 shorter events, 0.3 us)
Async XLA Ops:
  0.6 47.4 %copy-start = (bf16[8,512,128]{2,1,0:T(8,128)(2,1)S(1)}, bf16[8,512,128]{2,1,0:T(8,128)(2,1)}, u32[]{:S(2)}) copy-start(bf16[8,512,128]{2,1,0:T(8,128)(2,1)} %param.28) | copy-start | bytes 3145732
  3.4 72.0 %collective-permute-start = (bf16[2,14336]{1,0:T(2,128)(2,1)S(1)}, bf16[2,14336]{1,0:T(2,128)(2,1)S(1)}, u32[]{:S(2)}, u32[]{:S(2)}) collective-permute-start(bf16[2,14336]{1,0:T(2,128)(2,1)S(1)} %pad_maximum_fusion), channel_id=1, source_target_pairs={{0,24},{8,0},{16,8},{24,16},{1,25},{9,1},{17,9},{25,17},{2,26},{10... | collective-permute-start | bytes 172040 | tf_op jit(solution)/shard_map/ppermute | solution.py:31
  3.9 71.5 %collective-permute-start.1 = (bf16[2,14336]{1,0:T(2,128)(2,1)S(1)}, bf16[2,14336]{1,0:T(2,128)(2,1)S(1)}, u32[]{:S(2)}, u32[]{:S(2)}) collective-permute-start(bf16[2,14336]{1,0:T(2,128)(2,1)S(1)} %pad_maximum_fusion), channel_id=1, source_target_pairs={{0,16},{8,24},{16,0},{24,8},{1,17},{9,25},{17,1},{25,9},{2,18},{10... | collective-permute-start | bytes 172040 | tf_op jit(solution)/shard_map/ppermute | solution.py:31
  7.4 68.0 %collective-permute-start.2 = (bf16[2,14336]{1,0:T(2,128)(2,1)S(1)}, bf16[2,14336]{1,0:T(2,128)(2,1)S(1)}, u32[]{:S(2)}, u32[]{:S(2)}) collective-permute-start(bf16[2,14336]{1,0:T(2,128)(2,1)S(1)} %pad_maximum_fusion), channel_id=1, source_target_pairs={{0,8},{8,16},{16,24},{24,0},{1,9},{9,17},{17,25},{25,1},{2,10},{10... | collective-permute-start | bytes 172040 | tf_op jit(solution)/shard_map/ppermute | solution.py:31
  8.0 2.0 %copy-start.1 = (bf16[48,36864]{1,0:T(8,128)(2,1)S(1)}, bf16[48,36864]{1,0:T(8,128)(2,1)}, u32[]{:S(2)}) copy-start(bf16[48,36864]{1,0:T(8,128)(2,1)} %pages_ref.1) | copy-start | bytes 10616836
  10.0 1.7 copy-start.2
  11.7 0.7 copy-start.3
  12.4 0.7 copy-start.4
  13.1 0.7 copy-start.5
  13.7 35.2 %copy-start.6 = (bf16[1024,3584]{1,0:T(8,128)(2,1)S(1)}, bf16[1024,3584]{1,0:T(8,128)(2,1)}, u32[]{:S(2)}) copy-start(bf16[1024,3584]{1,0:T(8,128)(2,1)} %param.29) | copy-start | bytes 22020100
  51.0 23.1 %copy-start.9 = (s32[32,8]{0,1:T(8,128)S(1)}, s32[32,8]{0,1:T(8,128)}, u32[]{:S(2)}) copy-start(s32[32,8]{0,1:T(8,128)} %param.24) | copy-start | bytes 3076
  51.0 23.1 %copy-start.10 = (f32[32,8]{0,1:T(8,128)S(1)}, f32[32,8]{0,1:T(8,128)}, u32[]{:S(2)}) copy-start(f32[32,8]{0,1:T(8,128)} %param.25) | copy-start | bytes 3076
  51.0 23.2 %copy-start.11 = (s32[32]{0:T(128)S(1)}, s32[32]{0:T(128)}, u32[]{:S(2)}) copy-start(s32[32]{0:T(128)} %param.26) | copy-start | bytes 388
  51.1 24.9 %copy-start.7 = (bf16[8,14336]{1,0:T(8,128)(2,1)S(1)}, bf16[8,14336]{1,0:T(8,128)(2,1)}, u32[]{:S(2)}) copy-start(bf16[8,14336]{1,0:T(8,128)(2,1)} %param.18) | copy-start | bytes 688132
  66.7 10.8 %copy-start.8 = (f32[3584]{0:T(1024)S(1)}, f32[3584]{0:T(1024)}, u32[]{:S(2)}) copy-start(f32[3584]{0:T(1024)} %param.27) | copy-start | bytes 43012
